TPU v7x, 256 devices: a whole 4x4x8 slice. The times are simulated.
256 devices in a mesh: section: 4 (over x_hi, core), dp: 64 (over y, x_lo, z).
Axes of the slice: x: 4 (x_hi: 2, x_lo: 2; x = x_hi * 2 + x_lo), y: 4, z: 8, core: 2. Of those that a mesh axis runs over, the one named last changes fastest.
Arguments:
- activations: bfloat16 [12288, 8, 4096], P('dp', 'section'), may hold values from -8 to 8
- damping: float32 [8], P('section'), may hold values from 0.1 to 1
Outputs:
- schur_inverse: float32 [256, 128, 128], P(('section', 'dp'))
- coupling: float32 [256, 128, 128], P(('section', 'dp'))
All inputs are finite; a program needn't handle non-finite values.
Results may differ from a plain program's by a relative error of at most 0.0003.
Values may be sent and summed in bfloat16 or wider, within the bound.
A program may use at most 64 MiB of HBM per device.

v0:
```python
import jax
import jax.numpy as jnp
from jax import lax
from jax.sharding import PartitionSpec as P

B = 128


def passed_along(block, axis, distance):
    devices = range(lax.axis_size(axis))
    route = [(i - distance, i) for i in devices if i - distance in devices]
    return lax.ppermute(block, axis, route)


def sent_to_all(array, axis):
    copies = jnp.broadcast_to(array, (lax.axis_size(axis), *array.shape))
    return lax.all_to_all(copies, axis, split_axis=0, concat_axis=0, tiled=True)


def over_copies(array, axis):
    everything = sent_to_all(array, axis)
    return jnp.sum(everything, axis=0)


def solve_block(system, right_side):
    factor = jnp.linalg.cholesky(system)
    return jax.scipy.linalg.cho_solve((factor, True), right_side)


def local(activations, damping):
    token_rows, local_layers, model_width = activations.shape
    block_size = B
    blocks_layer = model_width // block_size
    group_size = lax.axis_size("dp")
    section_count = lax.axis_size("section")
    per_device = local_layers * blocks_layer // group_size
    tokens_all = token_rows * group_size
    flattened = activations.reshape(token_rows, local_layers * model_width)
    following_rows = passed_along(flattened[:, :model_width], "section", -1)
    next_layers = jnp.concatenate([flattened[:, model_width:], following_rows], axis=1)
    owner_layer = lax.axis_index("dp") * per_device // blocks_layer
    layer_index = jnp.arange(local_layers)
    sent_pairs = (
        flattened.reshape(token_rows, group_size, per_device * block_size),
        next_layers.reshape(token_rows, group_size, per_device * block_size),
    )
    left_cols, right_cols = (
        lax.all_to_all(sent_pairs[0], "dp", split_axis=1, concat_axis=0, tiled=True),
        lax.all_to_all(sent_pairs[1], "dp", split_axis=1, concat_axis=0, tiled=True),
    )
    diagonal_gram = (
        jnp.einsum("tgb,tgc->gbc", left_cols, left_cols, preferred_element_type=jnp.float32)
        / tokens_all
    )
    cross_gram = (
        jnp.einsum("tgb,tgc->gbc", left_cols, right_cols, preferred_element_type=jnp.float32)
        / tokens_all
    )
    owned_trace = jnp.sum(jnp.trace(diagonal_gram, axis1=1, axis2=2))
    traces = over_copies(jnp.where(layer_index == owner_layer, owned_trace, 0.0), "dp")
    identity = jnp.eye(block_size, dtype=jnp.float32)
    damp_level = jnp.sum(jnp.where(layer_index == owner_layer, traces * damping, 0.0)) / model_width
    damped = diagonal_gram + damp_level * identity
    following_damped = passed_along(damped, ("section", "dp"), -(group_size // local_layers))
    final_layer = jnp.logical_and(
        lax.axis_index("section") == section_count - 1, owner_layer == local_layers - 1
    )
    system = jnp.where(final_layer, identity, following_damped)
    cross_gram = jnp.where(final_layer, jnp.zeros_like(cross_gram), cross_gram)
    coupling_t = jax.vmap(solve_block)(system, jnp.swapaxes(cross_gram, 1, 2))
    schur = damped - jnp.matmul(cross_gram, coupling_t, precision=lax.Precision.HIGHEST)
    identities = jnp.broadcast_to(identity, schur.shape)
    schur_inverse = jax.vmap(solve_block)(schur, identities)
    return (schur_inverse, jnp.swapaxes(coupling_t, 1, 2))


def solution(mesh):
    placed = (P("dp", "section", None), P("section"))
    return jax.shard_map(
        local,
        mesh=mesh,
        in_specs=placed,
        out_specs=(P(("section", "dp"), None, None), P(("section", "dp"), None, None)),
        check_vma=False,
    )
```

profile of v0, /device:TPU:4, one launch (start us, length us, event | category | flops | bytes accessed | tf_op | source)
XLA Modules:
  0.0 224.7 jit_solution(8540265799306868774)
XLA Ops:
  0.6 4.8 %reshape_reshape.3 = bf16[192,64,128]{2,1,0:T(8,128)(2,1)S(1)} reshape(bf16[192,2,4096]{2,1,0:T(2,128)(2,1)} %param.5) | data formatting | bytes 6291456 | tf_op jit(solution)/shard_map/reshape;reshape | solution.py:44
  5.4 3.7 %copy.26 = bf16[192,64,128]{2,0,1:T(8,128)(2,1)} copy(bf16[192,64,128]{2,1,0:T(8,128)(2,1)S(1)} %reshape_reshape.3) | data formatting | bytes 6291456 | tf_op jit(solution)/shard_map/reshape;reshape | solution.py:44
  9.2 13.2 %all-to-all-start = ((bf16[192,64,128]{2,0,1:T(8,128)(2,1)}), bf16[192,64,128]{2,0,1:T(8,128)(2,1)}, u32[]{:S(2)}, u32[]{:S(2)}) async-start(bf16[192,64,128]{2,0,1:T(8,128)(2,1)} %copy.26), calls=%async_computation | async-start | bytes 6291456 | tf_op jit(solution)/shard_map/all_to_all | solution.py:48
  22.4 2.1 copy.42
  24.7 1.9 collective-permute-start
  26.7 70.0 %all-to-all-done = bf16[192,64,128]{2,0,1:T(8,128)(2,1)} async-done(((bf16[192,64,128]{2,0,1:T(8,128)(2,1)}), bf16[192,64,128]{2,0,1:T(8,128)(2,1)}, u32[]{:S(2)}, u32[]{:S(2)}) %all-to-all-start) | async-done | bytes 3145760 | tf_op jit(solution)/shard_map/all_to_all | solution.py:48
  96.7 4.5 %select_reduce_fusion.1 = (f32[]{:T(128)}, f32[128,128]{0,1:T(8,128)S(1)}) fusion(bf16[192,64,128]{2,0,1:T(8,128)(2,1)} %all-to-all-done), kind=kOutput, calls=%fused_computation.38 | convolution fusion | flops 402718720 | bytes 3211268 | tf_op jit(solution)/shard_map/tgb,tgc->gbc/dot_general | solution.py:52
  101.2 0.6 compare_select_fusion.1
  102.5 5.5 %all-to-all-start.1 = ((f32[64,1,2]{2,1,0:T(1,128)}), f32[64,1,2]{2,1,0:T(1,128)S(1)}, u32[]{:S(2)}, u32[]{:S(2)}) async-start(f32[64,1,2]{2,1,0:T(1,128)} %broadcast_in_dim.31), calls=%async_computation.1 | async-start | bytes 65536 | tf_op jit(solution)/shard_map/all_to_all | solution.py:17
  108.0 4.0 %copy_bitcast_fusion = bf16[192,64,128]{2,0,1:T(8,128)(2,1)} fusion(bf16[192,4096]{1,0:T(8,128)(2,1)} %collective-permute-done, bf16[192,4096]{1,0:T(8,128)(2,1)S(1)} %get-tuple-element.12), kind=kLoop, calls=%fused_computation | loop fusion | flops 6291456 | bytes 6291456 | tf_op jit(solution)/shard_map/reshape | solution.py:45
  112.0 6.3 %all-to-all-done.1 = f32[64,1,2]{2,1,0:T(1,128)S(1)} async-done(((f32[64,1,2]{2,1,0:T(1,128)}), f32[64,1,2]{2,1,0:T(1,128)S(1)}, u32[]{:S(2)}, u32[]{:S(2)}) %all-to-all-start.1) | async-done | bytes 544 | tf_op jit(solution)/shard_map/all_to_all | solution.py:17
  118.4 5.0 %all-to-all-start.2 = ((bf16[192,64,128]{2,0,1:T(8,128)(2,1)}), bf16[192,64,128]{2,0,1:T(8,128)(2,1)S(1)}, u32[]{:S(2)}, u32[]{:S(2)}) async-start(bf16[192,64,128]{2,0,1:T(8,128)(2,1)} %copy_bitcast_fusion), calls=%async_computation.2 | async-start | bytes 6291456 | tf_op jit(solution)/shard_map/all_to_all | solution.py:49
  124.8 3.6 %collective-permute-start.1 = (f32[1,128,128]{1,2,0:T(8,128)S(1)}, f32[1,128,128]{1,2,0:T(8,128)S(1)}, u32[]{:S(2)}, u32[]{:S(2)}) collective-permute-start(f32[1,128,128]{1,2,0:T(8,128)S(1)} %fusion.39), channel_id=1, source_target_pairs={{32,0},{33,1},{34,2},{35,3},{36,4},{37,5},{38,6},{39,7},{40,8},{41... | collective-permute-start | bytes 196616 | tf_op jit(solution)/shard_map/ppermute | solution.py:12
  128.4 5.2 %collective-permute-done.1 = f32[1,128,128]{1,2,0:T(8,128)S(1)} collective-permute-done((f32[1,128,128]{1,2,0:T(8,128)S(1)}, f32[1,128,128]{1,2,0:T(8,128)S(1)}, u32[]{:S(2)}, u32[]{:S(2)}) %collective-permute-start.1) | collective-permute-done | bytes 65568 | tf_op jit(solution)/shard_map/ppermute | solution.py:12
  133.8 11.7 %custom-call.10 = f32[1,128,128]{2,1,0:T(8,128)S(1)} custom-call(f32[1,128,128]{2,1,0:T(8,128)S(1)} %fusion.36), custom_call_target="Cholesky" | custom-call | tf_op jit(solution)/shard_map/vmap(jit(cholesky))/cholesky | solution.py:26
  146.2 0.7 fusion.26
  146.9 9.8 %custom-call.11 = f32[1,1,128,128]{2,3,1,0:T(8,128)S(1)} custom-call(f32[1,1,128,128]{3,2,1,0:T(8,128)S(1)} %fusion.26), custom_call_target="InvertDiagBlocksLowerTriangular" | custom-call | tf_op jit(solution)/shard_map/vmap(jit(_cho_solve))/triangular_solve | solution.py:27
  156.7 39.4 %all-to-all-done.2 = bf16[192,64,128]{2,0,1:T(8,128)(2,1)S(1)} async-done(((bf16[192,64,128]{2,0,1:T(8,128)(2,1)}), bf16[192,64,128]{2,0,1:T(8,128)(2,1)S(1)}, u32[]{:S(2)}, u32[]{:S(2)}) %all-to-all-start.2) | async-done | bytes 3145760 | tf_op jit(solution)/shard_map/all_to_all | solution.py:49
  196.1 3.0 %fusion.21 = f32[128,128]{0,1:T(8,128)S(1)} fusion(bf16[192,64,128]{2,0,1:T(8,128)(2,1)} %all-to-all-done, bf16[192,64,128]{2,0,1:T(8,128)(2,1)S(1)} %all-to-all-done.2, pred[]{:T(512)S(6)} %and.11), kind=kOutput, calls=%fused_computation.13 | convolution fusion | flops 402685952 | bytes 6356993 | tf_op jit(solution)/shard_map/tgb,tgc->gbc/dot_general | solution.py:56
  200.0 11.7 %custom-call.12 = f32[1,128,128]{2,1,0:T(8,128)S(1)} custom-call(f32[1,128,128]{2,1,0:T(8,128)S(1)} %fusion.29), custom_call_target="Cholesky" | custom-call | tf_op jit(solution)/shard_map/vmap(jit(cholesky))/cholesky | solution.py:26
  212.4 0.7 fusion.27
  213.1 9.8 %custom-call.13 = f32[1,1,128,128]{2,3,1,0:T(8,128)S(1)} custom-call(f32[1,1,128,128]{3,2,1,0:T(8,128)S(1)} %fusion.27), custom_call_target="InvertDiagBlocksLowerTriangular" | custom-call | tf_op jit(solution)/shard_map/vmap(jit(_cho_solve))/triangular_solve | solution.py:27
  223.2 0.8 convolution_bitcast_fusion
  224.0 0.7 copy.34
  (23 shorter events, 4.2 us)
Async XLA Ops:
  9.2 13.2 %copy-start = (bf16[192,2,4096]{2,1,0:T(2,128)(2,1)S(1)}, bf16[192,2,4096]{2,1,0:T(2,128)(2,1)}, u32[]{:S(2)}) copy-start(bf16[192,2,4096]{2,1,0:T(2,128)(2,1)} %param.5) | copy-start | bytes 9437188
  9.2 87.5 %all-to-all-start = ((bf16[192,64,128]{2,0,1:T(8,128)(2,1)}), bf16[192,64,128]{2,0,1:T(8,128)(2,1)}, u32[]{:S(2)}, u32[]{:S(2)}) async-start(bf16[192,64,128]{2,0,1:T(8,128)(2,1)} %copy.26), calls=%async_computation | async-start | bytes 6291456 | tf_op jit(solution)/shard_map/all_to_all | solution.py:48
  24.7 83.3 %collective-permute-start = (bf16[192,4096]{1,0:T(8,128)(2,1)S(1)}, bf16[192,4096]{1,0:T(8,128)(2,1)}, u32[]{:S(2)}, u32[]{:S(2)}) collective-permute-start(bf16[192,4096]{1,0:T(8,128)(2,1)S(1)} %get-tuple-element.13), channel_id=1, source_target_pairs={{64,0},{128,64},{192,128},{65,1},{129,65},{193,129},{66,2},{130,66... | collective-permute-start | bytes 4718600 | tf_op jit(solution)/shard_map/ppermute | solution.py:12
  102.5 15.9 %all-to-all-start.1 = ((f32[64,1,2]{2,1,0:T(1,128)}), f32[64,1,2]{2,1,0:T(1,128)S(1)}, u32[]{:S(2)}, u32[]{:S(2)}) async-start(f32[64,1,2]{2,1,0:T(1,128)} %broadcast_in_dim.31), calls=%async_computation.1 | async-start | bytes 65536 | tf_op jit(solution)/shard_map/all_to_all | solution.py:17
  112.0 11.5 %copy-start.1 = (f32[2]{0:T(128)S(1)}, f32[2]{0:T(128)}, u32[]{:S(2)}) copy-start(f32[2]{0:T(128)} %param.6) | copy-start | bytes 28
  118.4 77.8 %all-to-all-start.2 = ((bf16[192,64,128]{2,0,1:T(8,128)(2,1)}), bf16[192,64,128]{2,0,1:T(8,128)(2,1)S(1)}, u32[]{:S(2)}, u32[]{:S(2)}) async-start(bf16[192,64,128]{2,0,1:T(8,128)(2,1)} %copy_bitcast_fusion), calls=%async_computation.2 | async-start | bytes 6291456 | tf_op jit(solution)/shard_map/all_to_all | solution.py:49
  124.8 8.9 %collective-permute-start.1 = (f32[1,128,128]{1,2,0:T(8,128)S(1)}, f32[1,128,128]{1,2,0:T(8,128)S(1)}, u32[]{:S(2)}, u32[]{:S(2)}) collective-permute-start(f32[1,128,128]{1,2,0:T(8,128)S(1)} %fusion.39), channel_id=1, source_target_pairs={{32,0},{33,1},{34,2},{35,3},{36,4},{37,5},{38,6},{39,7},{40,8},{41... | collective-permute-start | bytes 196616 | tf_op jit(solution)/shard_map/ppermute | solution.py:12
where the time goes:
time: 225 us
  waiting for transfers between devices  121 us (54%)
  other arithmetic  51.1 us (23%)
  starting transfers between devices  29.4 us (13%)
  local copies, waits for them, and re-layouts  12.4 us (6%)
  matrix products  9.39 us (4%)
    all_to_all x1, waiting for transfers between devices, local(): lax.all_to_all(sent_pairs[0], 'dp', split_axis=1, concat_axis=0, tiled=True)  70 us
    all_to_all x1, waiting for transfers between devices, local(): lax.all_to_all(sent_pairs[1], 'dp', split_axis=1, concat_axis=0, tiled=True)  39.4 us
    another operation x6, other arithmetic, solve_block(): factor = jnp.linalg.cholesky(system)  24.8 us
    another operation x4, other arithmetic, solve_block(): return jax.scipy.linalg.cho_solve((factor, True), right_side)  20.9 us
    all_to_all x1, starting transfers between devices, local(): lax.all_to_all(sent_pairs[0], 'dp', split_axis=1, concat_axis=0, tiled=True)  13.2 us
    another operation x2, local copies, waits for them, and re-layouts, local(): flattened.reshape(token_rows, group_size, per_device * block_size)  8.53 us
    all_to_all x1, waiting for transfers between devices, sent_to_all(): return lax.all_to_all(copies, axis, split_axis=0, concat_axis=0, tiled=True)  6.34 us
    ppermute x2, starting transfers between devices, passed_along(): return lax.ppermute(block, axis, route)  5.55 us
  transfers between devices with their start and end apart: 5, of which 4 were waited for; matrix products, arithmetic and copies ran while one was open for 16% of the time, Pallas kernels for 0%

commit v1 on v0

--- a/solution.py
+++ b/solution.py
@@ -46,7 +46,12 @@
     )
     left_cols, right_cols = (
         lax.all_to_all(sent_pairs[0], "dp", split_axis=1, concat_axis=0, tiled=True),
-        lax.all_to_all(sent_pairs[1], "dp", split_axis=1, concat_axis=0, tiled=True),
+        jnp.concatenate(
+            lax.all_to_all(
+                jnp.stack(jnp.split(sent_pairs[1], lax.axis_size("dp"), axis=1)), "dp", 0, 0
+            ),
+            axis=0,
+        ),
     )
     diagonal_gram = (
         jnp.einsum("tgb,tgc->gbc", left_cols, left_cols, preferred_element_type=jnp.float32)

time: 225 us -> 234 us (1.040)
  local copies, waits for them, and re-layouts: 12.4 us -> 64.6 us
  waiting for transfers between devices: 121 us -> 80 us
  matrix products: 9.39 us -> 6.43 us
    all_to_all x1, waiting for transfers between devices: 70 us -> 26.7 us  [local(): lax.all_to_all(sent_pairs[0], 'dp', split_axis=1, concat_axis=0, tiled=True)]
    unnamed x6 -> x70, local copies, waits for them, and re-layouts: 2.82 us -> 44.8 us
    split x0 -> x4, local copies, waits for them, and re-layouts: none -> 6.49 us  [local(): jnp.split(sent_pairs[1], lax.axis_size('dp'), axis=1)]
    reshape x1 -> x0, other arithmetic: 4 us -> none  [local(): next_layers.reshape(token_rows, group_size, per_device * block_size)]
    all_to_all x1, waiting for transfers between devices: 6.34 us -> 9.72 us  [sent_to_all(): return lax.all_to_all(copies, axis, split_axis=0, concat_axis=0, tiled=True)]
    dot_general x1, matrix products: 4.51 us -> 1.62 us  [local(): jnp.einsum('tgb,tgc->gbc', left_cols, left_cols, preferred_element_type=j...]
  transfers between devices with their start and end apart: 5 -> 5, of which waited for: 4 -> 4; matrix products, arithmetic and copies ran while one was open for 16% -> 36% of each run, Pallas kernels for 0% -> 0%
where the time goes in v1:
time: 234 us; the launch traced here: 233 us
  waiting for transfers between devices  80 us (34%)
  local copies, waits for them, and re-layouts  64.6 us (28%)
  other arithmetic  49.2 us (21%)
  starting transfers between devices  30.7 us (13%)
  matrix products  6.43 us (3%)
    unnamed x70, local copies, waits for them, and re-layouts  44.8 us
    all_to_all x1, waiting for transfers between devices, local(): lax.all_to_all(jnp.stack(jnp.split(sent_pairs[1], lax.axis_size('dp'), ax...  39.2 us
    all_to_all x1, waiting for transfers between devices, local(): lax.all_to_all(sent_pairs[0], 'dp', split_axis=1, concat_axis=0, tiled=True)  26.7 us
    another operation x6, other arithmetic, solve_block(): factor = jnp.linalg.cholesky(system)  24.8 us
    another operation x4, other arithmetic, solve_block(): return jax.scipy.linalg.cho_solve((factor, True), right_side)  20.9 us
    all_to_all x1, starting transfers between devices, local(): lax.all_to_all(sent_pairs[0], 'dp', split_axis=1, concat_axis=0, tiled=True)  13.8 us
    all_to_all x1, waiting for transfers between devices, sent_to_all(): return lax.all_to_all(copies, axis, split_axis=0, concat_axis=0, tiled=True)  9.72 us
    another operation x2, local copies, waits for them, and re-layouts, local(): flattened.reshape(token_rows, group_size, per_device * block_size)  9.62 us
  transfers between devices with their start and end apart: 5, of which 4 were waited for; matrix products, arithmetic and copies ran while one was open for 36% of the time, Pallas kernels for 0%

profile of v1, /device:TPU:4, one launch (start us, length us, event | category | flops | bytes accessed | tf_op | source)
XLA Modules:
  0.0 232.6 jit_solution(6855993180507538318)
XLA Ops:
  0.6 4.0 %copy.1862 = bf16[24,8,2,4096]{3,1,2,0:T(8,128)(2,1)S(1)} copy(bf16[24,8,2,4096]{3,2,1,0:T(2,128)(2,1)} %bitcast.222) | data formatting | bytes 6291456
  4.6 2.1 fusion.45
  6.7 2.0 collective-permute-start
  8.7 4.0 %reshape_reshape.3 = bf16[192,64,128]{2,1,0:T(8,128)(2,1)} reshape(bf16[192,2,4096]{2,1,0:T(2,128)(2,1)S(1)} %copy-done) | data formatting | bytes 6291456 | tf_op jit(solution)/shard_map/reshape;reshape | solution.py:44
  12.8 5.6 %copy.1789 = bf16[192,64,128]{2,0,1:T(8,128)(2,1)} copy(bf16[192,64,128]{2,1,0:T(8,128)(2,1)} %reshape_reshape.3) | data formatting | bytes 6291456 | tf_op jit(solution)/shard_map/reshape;reshape | solution.py:44
  18.4 13.8 %all-to-all-start = ((bf16[192,64,128]{2,0,1:T(8,128)(2,1)}), bf16[192,64,128]{2,0,1:T(8,128)(2,1)S(1)}, u32[]{:S(2)}, u32[]{:S(2)}) async-start(bf16[192,64,128]{2,0,1:T(8,128)(2,1)} %copy.1789), calls=%async_computation | async-start | bytes 6291456 | tf_op jit(solution)/shard_map/all_to_all | solution.py:48
  32.1 2.1 maximum_bitcast_fusion
  34.2 0.9 copy.1863
  35.6 2.0 fusion.43
  37.6 2.0 fusion.42
  67.6 2.0 fusion.41
  80.9 26.7 %all-to-all-done = bf16[192,64,128]{2,0,1:T(8,128)(2,1)S(1)} async-done(((bf16[192,64,128]{2,0,1:T(8,128)(2,1)}), bf16[192,64,128]{2,0,1:T(8,128)(2,1)S(1)}, u32[]{:S(2)}, u32[]{:S(2)}) %all-to-all-start) | async-done | bytes 3145760 | tf_op jit(solution)/shard_map/all_to_all | solution.py:48
  107.5 1.6 select_reduce_fusion.1
  110.5 5.3 %all-to-all-start.1 = ((f32[64,1,2]{2,1,0:T(1,128)}), f32[64,1,2]{2,1,0:T(1,128)S(1)}, u32[]{:S(2)}, u32[]{:S(2)}) async-start(f32[64,1,2]{2,1,0:T(1,128)} %broadcast_in_dim.31), calls=%async_computation.1 | async-start | bytes 65536 | tf_op jit(solution)/shard_map/all_to_all | solution.py:17
  116.4 9.7 %all-to-all-done.1 = f32[64,1,2]{2,1,0:T(1,128)S(1)} async-done(((f32[64,1,2]{2,1,0:T(1,128)}), f32[64,1,2]{2,1,0:T(1,128)S(1)}, u32[]{:S(2)}, u32[]{:S(2)}) %all-to-all-start.1) | async-done | bytes 544 | tf_op jit(solution)/shard_map/all_to_all | solution.py:17
  126.1 5.6 %all-to-all-start.2 = ((bf16[64,192,1,128]{3,1,2,0:T(8,128)(2,1)}), bf16[64,192,1,128]{3,1,2,0:T(8,128)(2,1)}, u32[]{:S(2)}, u32[]{:S(2)}) async-start(bf16[64,192,1,128]{3,1,2,0:T(8,128)(2,1)} %constant_dynamic-update-slice_fusion), calls=%async_computation.2 | async-start | bytes 6291456 | tf_op jit(solution)/shard_map/all_to_all | solution.py:50
  133.2 4.0 %collective-permute-start.1 = (f32[1,128,128]{1,2,0:T(8,128)S(1)}, f32[1,128,128]{1,2,0:T(8,128)S(1)}, u32[]{:S(2)}, u32[]{:S(2)}) collective-permute-start(f32[1,128,128]{1,2,0:T(8,128)S(1)} %bitcast.227), channel_id=1, source_target_pairs={{32,0},{33,1},{34,2},{35,3},{36,4},{37,5},{38,6},{39,7},{40,8},{41... | collective-permute-start | bytes 196616 | tf_op jit(solution)/shard_map/ppermute | solution.py:12
  137.2 4.5 %collective-permute-done.1 = f32[1,128,128]{1,2,0:T(8,128)S(1)} collective-permute-done((f32[1,128,128]{1,2,0:T(8,128)S(1)}, f32[1,128,128]{1,2,0:T(8,128)S(1)}, u32[]{:S(2)}, u32[]{:S(2)}) %collective-permute-start.1) | collective-permute-done | bytes 65568 | tf_op jit(solution)/shard_map/ppermute | solution.py:12
  141.8 11.7 %custom-call.10 = f32[1,128,128]{2,1,0:T(8,128)S(1)} custom-call(f32[1,128,128]{2,1,0:T(8,128)S(1)} %fusion.37), custom_call_target="Cholesky" | custom-call | tf_op jit(solution)/shard_map/vmap(jit(cholesky))/cholesky | solution.py:26
  154.9 9.8 %custom-call.11 = f32[1,1,128,128]{2,3,1,0:T(8,128)S(1)} custom-call(f32[1,1,128,128]{3,2,1,0:T(8,128)S(1)} %fusion.26), custom_call_target="InvertDiagBlocksLowerTriangular" | custom-call | tf_op jit(solution)/shard_map/vmap(jit(_cho_solve))/triangular_solve | solution.py:27
  164.7 39.2 %all-to-all-done.2 = bf16[64,192,1,128]{3,1,2,0:T(8,128)(2,1)} async-done(((bf16[64,192,1,128]{3,1,2,0:T(8,128)(2,1)}), bf16[64,192,1,128]{3,1,2,0:T(8,128)(2,1)}, u32[]{:S(2)}, u32[]{:S(2)}) %all-to-all-start.2) | async-done | bytes 3145760 | tf_op jit(solution)/shard_map/all_to_all | solution.py:50
  203.9 2.9 %fusion.21 = f32[128,128]{1,0:T(8,128)S(1)} fusion(bf16[192,64,128]{2,0,1:T(8,128)(2,1)S(1)} %all-to-all-done, bf16[64,192,1,128]{3,1,2,0:T(8,128)(2,1)} %all-to-all-done.2, pred[]{:T(512)S(6)} %and.11), kind=kOutput, calls=%fused_computation.12 | convolution fusion | flops 402685952 | bytes 6356993 | tf_op jit(solution)/shard_map/tgb,tgc->gbc/dot_general | solution.py:61
  207.9 11.7 %custom-call.12 = f32[1,128,128]{2,1,0:T(8,128)S(1)} custom-call(f32[1,128,128]{2,1,0:T(8,128)S(1)} %fusion.29), custom_call_target="Cholesky" | custom-call | tf_op jit(solution)/shard_map/vmap(jit(cholesky))/cholesky | solution.py:26
  220.9 9.8 %custom-call.13 = f32[1,1,128,128]{2,3,1,0:T(8,128)S(1)} custom-call(f32[1,1,128,128]{3,2,1,0:T(8,128)S(1)} %fusion.27), custom_call_target="InvertDiagBlocksLowerTriangular" | custom-call | tf_op jit(solution)/shard_map/vmap(jit(_cho_solve))/triangular_solve | solution.py:27
  (95 shorter events, 48.1 us)
Async XLA Ops:
  4.6 4.1 %copy-start = (bf16[192,2,4096]{2,1,0:T(2,128)(2,1)S(1)}, bf16[192,2,4096]{2,1,0:T(2,128)(2,1)}, u32[]{:S(2)}) copy-start(bf16[192,2,4096]{2,1,0:T(2,128)(2,1)} %param.5) | copy-start | bytes 9437188
  6.7 25.5 %collective-permute-start = (bf16[192,4096]{1,0:T(8,128)(2,1)}, bf16[192,4096]{1,0:T(8,128)(2,1)}, u32[]{:S(2)}, u32[]{:S(2)}) collective-permute-start(bf16[192,4096]{1,0:T(8,128)(2,1)} %get-tuple-element.139), channel_id=1, source_target_pairs={{64,0},{128,64},{192,128},{65,1},{129,65},{193,129},{66,2},{130,66... | collective-permute-start | bytes 4718600 | tf_op jit(solution)/shard_map/ppermute | solution.py:12
  18.4 89.2 %all-to-all-start = ((bf16[192,64,128]{2,0,1:T(8,128)(2,1)}), bf16[192,64,128]{2,0,1:T(8,128)(2,1)S(1)}, u32[]{:S(2)}, u32[]{:S(2)}) async-start(bf16[192,64,128]{2,0,1:T(8,128)(2,1)} %copy.1789), calls=%async_computation | async-start | bytes 6291456 | tf_op jit(solution)/shard_map/all_to_all | solution.py:48
  110.5 15.7 %all-to-all-start.1 = ((f32[64,1,2]{2,1,0:T(1,128)}), f32[64,1,2]{2,1,0:T(1,128)S(1)}, u32[]{:S(2)}, u32[]{:S(2)}) async-start(f32[64,1,2]{2,1,0:T(1,128)} %broadcast_in_dim.31), calls=%async_computation.1 | async-start | bytes 65536 | tf_op jit(solution)/shard_map/all_to_all | solution.py:17
  116.4 15.4 %copy-start.1 = (f32[2]{0:T(128)S(1)}, f32[2]{0:T(128)}, u32[]{:S(2)}) copy-start(f32[2]{0:T(128)} %param.6) | copy-start | bytes 28
  126.1 77.7 %all-to-all-start.2 = ((bf16[64,192,1,128]{3,1,2,0:T(8,128)(2,1)}), bf16[64,192,1,128]{3,1,2,0:T(8,128)(2,1)}, u32[]{:S(2)}, u32[]{:S(2)}) async-start(bf16[64,192,1,128]{3,1,2,0:T(8,128)(2,1)} %constant_dynamic-update-slice_fusion), calls=%async_computation.2 | async-start | bytes 6291456 | tf_op jit(solution)/shard_map/all_to_all | solution.py:50
  133.2 8.5 %collective-permute-start.1 = (f32[1,128,128]{1,2,0:T(8,128)S(1)}, f32[1,128,128]{1,2,0:T(8,128)S(1)}, u32[]{:S(2)}, u32[]{:S(2)}) collective-permute-start(f32[1,128,128]{1,2,0:T(8,128)S(1)} %bitcast.227), channel_id=1, source_target_pairs={{32,0},{33,1},{34,2},{35,3},{36,4},{37,5},{38,6},{39,7},{40,8},{41... | collective-permute-start | bytes 196616 | tf_op jit(solution)/shard_map/ppermute | solution.py:12
